TPU v7x, 32 devices: a whole 2x2x4 slice. The times are simulated.
32 devices in a mesh: fourier: 2 (over x), ex: 4 (over z), ey: 4 (over y, core).
Axes of the slice: x: 2, y: 2, z: 4, core: 2. Of those that a mesh axis runs over, the one named last changes fastest.
Arguments:
- forcing: float32 [128, 81, 2048], P('fourier', None, ('ex', 'ey')), may hold values from -6 to 6
- element_coef: float32 [2048], P(('ex', 'ey')), may hold values from 0.5 to 2
- schur: float32 [128, 32, 32], P('fourier'), may hold values from -12 to 20, as said below
- couple: float32 [128, 32, 49], P('fourier'), may hold values from -0.875 to 0.875
- inner_inv: float32 [128, 49, 49], P('fourier'), may hold values from -3 to 4.5, as said below
- element_cell: int32 [2048], P(('ex', 'ey')), may hold values from 0 to 127, as said below
Outputs:
- velocity: float32 [128, 81, 2048], P('fourier', None, ('ex', 'ey'))
Inputs may be any that keep to these rules, and one draw needn't show every extreme that they name: `element_cell`: each aligned block of 128 entries is a permutation of 0 to 127. `schur`: each matrix is symmetric positive definite. `inner_inv`: each matrix is symmetric positive definite.
All inputs are finite; a program needn't handle non-finite values.
Results may differ from a plain program's by a relative error of at most 0.0001.
Values sent between devices are 32-bit elements; how exact they have to be, the bound alone decides.
A program may use at most 128 MiB of HBM per device.

v0:
```python
import functools
import math

import jax
import jax.numpy as jnp
import numpy as np
from jax import lax
from jax.experimental import pallas as pl
from jax.experimental.pallas import tpu as pltpu
from jax.sharding import PartitionSpec as P

P_SIZE = 8
ITERS = 3
ELX = 8
ELY = 16
NB = 4 * P_SIZE
HIGH = lax.Precision.HIGH
HIGHEST = lax.Precision.HIGHEST


def dft_rows(length):
    row_index = jnp.arange(length)[:, None]
    plane_pos = jnp.arange(length, dtype=jnp.float32)[None, :]
    waves = ((row_index + 1) // 2).astype(jnp.float32)
    angles = 2.0 * math.pi * waves * plane_pos / length
    factor = math.sqrt(2.0 / length)
    result = jnp.where(row_index % 2 == 1, factor * jnp.cos(angles), factor * jnp.sin(angles))
    result = jnp.where(row_index == 0, 1.0 / math.sqrt(length), result)
    result = jnp.where(
        row_index == length - 1, jnp.cos(math.pi * plane_pos) / math.sqrt(length), result
    )
    return result


def node_masks():
    slots = np.arange(NB)[:, None]
    cells = jnp.arange(ELX * ELY)[None, :]
    row_ids = lax.axis_index("ex") * ELX + cells // ELY
    col_ids = lax.axis_index("ey") * ELY + cells % ELY
    rows_total = ELX * lax.axis_size("ex")
    cols_total = ELY * lax.axis_size("ey")
    on_left = jnp.asarray((slots == 0) | (slots >= 3 * P_SIZE))
    on_right = jnp.asarray((slots >= P_SIZE) & (slots <= 2 * P_SIZE))
    on_bottom = jnp.asarray(slots <= P_SIZE)
    on_top = jnp.asarray((slots >= 2 * P_SIZE) & (slots <= 3 * P_SIZE))
    dropped = (
        on_left & (row_ids == 0)
        | on_right & (row_ids == rows_total - 1)
        | on_bottom & (col_ids == 0)
        | on_top & (col_ids == cols_total - 1)
    )
    keep = jnp.where(dropped, 0.0, 1.0).astype(jnp.float32)
    corner_weight = jnp.asarray(np.where(slots % P_SIZE == 0, 0.25, 0.5).astype(np.float32))
    return keep, keep * corner_weight


def split_high_low(values):
    high = lax.reduce_precision(values, 8, 7)
    return high.astype(jnp.bfloat16), (values - high).astype(jnp.bfloat16)


def cg_kernel(
    modes,
    cond_ref,
    schur_ref,
    scale_ref,
    keep_ref,
    weight_ref,
    x_ref,
    res_ref,
    app_ref,
    dir_ref,
    along_ref,
    xs_ref,
    xr_ref,
    ys_ref,
    yr_ref,
    ps_ref,
    pr_ex,
    pr_ey,
    halo_send,
    halo_recv,
    sum_send_ex,
    sum_recv_ex,
    sum_send_ey,
    sum_recv_ey,
):
    cells = cond_ref.shape[1]
    sizes = {axis: lax.axis_size(axis) for axis in ("ex", "ey")}
    place = {axis: lax.axis_index(axis) for axis in ("ex", "ey")}
    lane = lax.broadcasted_iota(jnp.int32, (modes, cells), 1)
    lane_row = lane // ELY
    lane_col = lane % ELY

    def node(n):
        if isinstance(n, int):
            return pl.ds(n * modes, modes)
        return pl.ds(pl.multiple_of(n * modes, modes), modes)

    def turned(value, shift):
        shift = shift % cells
        return pltpu.roll(value, shift, 1) if shift else value

    xr_ref[...] = jnp.zeros_like(xr_ref)
    yr_ref[...] = jnp.zeros_like(yr_ref)

    barrier = pltpu.get_barrier_semaphore()
    for axis in ("ex", "ey"):
        for hop in range(1, sizes[axis]):
            pl.semaphore_signal(
                barrier,
                inc=1,
                device_id={axis: lax.rem(place[axis] + hop, sizes[axis])},
                device_id_type=pl.DeviceIdType.MESH,
            )
    for ex_step in (1, -1):
        for ey_step in (1, -1):
            pl.semaphore_signal(
                barrier,
                inc=1,
                device_id={
                    "ex": lax.rem(place["ex"] + ex_step + sizes["ex"], sizes["ex"]),
                    "ey": lax.rem(place["ey"] + ey_step + sizes["ey"], sizes["ey"]),
                },
                device_id_type=pl.DeviceIdType.MESH,
            )
    pl.semaphore_wait(barrier, sizes["ex"] + sizes["ey"] + 2)

    def exists(axis, step):
        if step == 0:
            return None
        return place[axis] < sizes[axis] - 1 if step > 0 else place[axis] > 0

    def guarded(ex_step, ey_step, action):
        tests = [t for t in (exists("ex", ex_step), exists("ey", ey_step)) if t is not None]
        pl.when(functools.reduce(jnp.logical_and, tests))(action)

    def halo_copy(turn, number, source, target, ex_step, ey_step):
        copy = pltpu.make_async_remote_copy(
            src_ref=source,
            dst_ref=target,
            send_sem=halo_send.at[turn, number],
            recv_sem=halo_recv.at[turn, number],
            device_id={
                "ex": lax.rem(place["ex"] + ex_step + sizes["ex"], sizes["ex"]),
                "ey": lax.rem(place["ey"] + ey_step + sizes["ey"], sizes["ey"]),
            },
            device_id_type=pl.DeviceIdType.MESH,
        )
        guarded(ex_step, ey_step, copy.start)

        def arrive():
            guarded(-ex_step, -ey_step, copy.wait_recv)

        def leave():
            guarded(ex_step, ey_step, copy.wait_send)

        return arrive, leave

    def assemble(ref, turn):
        bottom = lambda k: k
        top = lambda k: 3 * P_SIZE - k
        up = jnp.zeros((modes, cells), jnp.float32)
        down = up
        for k in range(P_SIZE + 1):
            up = jnp.where(lane_col == k, turned(ref[node(top(k)), :], k - ELY + 1), up)
            down = jnp.where(lane_col == k, turned(ref[node(bottom(k)), :], k), down)
        ys_ref[turn, 0] = up
        ys_ref[turn, 1] = down
        copies = []
        for slot, ex_step in ((1, 1), (2, -1), (0, 0)):
            for way, ey_step in ((0, 1), (1, -1)):
                copies.append(
                    halo_copy(
                        turn,
                        2 * slot + way,
                        ys_ref.at[turn, way],
                        yr_ref.at[turn, slot, way],
                        ex_step,
                        ey_step,
                    )
                )

        left = lambda k: (NB - k) % NB
        right = lambda k: P_SIZE + k
        last = cells - ELY
        up = jnp.zeros((modes, cells), jnp.float32)
        down = up
        for k in range(P_SIZE):
            up = jnp.where(lane_row == k, turned(ref[node(right(k)), :], ELY * k - last), up)
            down = jnp.where(lane_row == k, turned(ref[node(left(k)), :], ELY * k), down)
        xs_ref[turn, 0, 0] = up
        xs_ref[turn, 1, 0] = down
        xs_ref[turn, 0, 1] = turned(ref[node(right(P_SIZE)), :], -last)
        xs_ref[turn, 1, 1] = ref[node(left(P_SIZE)), :]
        for way, ex_step in ((0, 1), (1, -1)):
            copies.append(
                halo_copy(turn, 6 + way, xs_ref.at[turn, way], xr_ref.at[turn, way], ex_step, 0)
            )

        for k in range(P_SIZE + 1):
            here_left, here_right = ref[node(left(k)), :], ref[node(right(k)), :]
            ref[node(left(k)), :] = here_left + jnp.where(
                lane_row == 0, 0.0, turned(here_right, ELY)
            )
            ref[node(right(k)), :] = here_right + jnp.where(
                lane_row == ELX - 1, 0.0, turned(here_left, -ELY)
            )
        for arrive, _ in copies:
            arrive()

        for k in range(P_SIZE + 1):
            part, lanes = divmod(k, P_SIZE)
            low = turned(xr_ref[turn, 0, part], -ELY * lanes)
            high = turned(xr_ref[turn, 1, part], last - ELY * lanes)
            for n, halo, row in ((left(k), low, 0), (right(k), high, ELX - 1)):
                value = ref[node(n), :] + jnp.where(lane_row == row, halo, 0.0)
                if n % (2 * P_SIZE) > P_SIZE:
                    value = value * keep_ref[n : n + 1, :]
                ref[node(n), :] = value

        lines = []
        for way in range(2):
            line = yr_ref[turn, 0, way]
            before = jnp.where(
                lane == 0, turned(yr_ref[turn, 1, way], P_SIZE), turned(line, P_SIZE)
            )
            after = jnp.where(
                lane == last + P_SIZE, turned(yr_ref[turn, 2, way], -P_SIZE), turned(line, -P_SIZE)
            )
            lines.append(
                line
                + jnp.where(lane_col == 0, before, jnp.where(lane_col == P_SIZE, after, 0.0))
            )
        low_all, high_all = lines
        for k in range(P_SIZE + 1):
            b, t = bottom(k), top(k)
            here_bottom, here_top = ref[node(b), :], ref[node(t), :]
            ref[node(b), :] = keep_ref[b : b + 1, :] * (
                here_bottom
                + jnp.where(lane_col == 0, turned(low_all, -k), turned(here_top, 1))
            )
            ref[node(t), :] = keep_ref[t : t + 1, :] * (
                here_top
                + jnp.where(
                    lane_col == ELY - 1, turned(high_all, ELY - 1 - k), turned(here_bottom, -1)
                )
            )
        for _, leave in copies:
            leave()

    def operator(turn):
        scale = scale_ref[0:1, :]
        block = 8

        def step(outer, carry):
            for inner in range(block):
                mode = outer * block + inner
                value = res_ref[pl.ds(mode, NB, stride=modes), :]
                high = value.astype(jnp.bfloat16)
                low = (value - high.astype(jnp.float32)).astype(jnp.bfloat16)
                image = jnp.dot(
                    schur_ref[mode],
                    jnp.concatenate([high, low, high], 0),
                    preferred_element_type=jnp.float32,
                )
                app_ref[pl.ds(mode, NB, stride=modes), :] = image * scale
            return carry

        lax.fori_loop(0, modes // block, step, 0)
        assemble(app_ref, turn)

    def group_sum(mine, axis, turn, stage, slots, send_sem, recv_sem):
        ps_ref[turn, stage] = mine
        copies = [
            pltpu.make_async_remote_copy(
                src_ref=ps_ref.at[turn, stage],
                dst_ref=slots.at[turn, hop - 1],
                send_sem=send_sem.at[turn, hop - 1],
                recv_sem=recv_sem.at[turn, hop - 1],
                device_id={axis: lax.rem(place[axis] + hop, sizes[axis])},
                device_id_type=pl.DeviceIdType.MESH,
            )
            for hop in range(1, sizes[axis])
        ]
        for copy in copies:
            copy.start()
        for hop, copy in enumerate(copies):
            copy.wait_recv()
            mine = mine + slots[turn, hop]
        for copy in copies:
            copy.wait_send()
        return mine

    def paired(turn):
        def step(n, sums):
            weighted = weight_ref[pl.ds(n, 1), :] * res_ref[node(n), :]
            return (
                sums[0] + weighted * res_ref[node(n), :],
                sums[1] + weighted * app_ref[node(n), :],
            )

        zero = jnp.zeros((modes, cells), jnp.float32)
        norm, curve = lax.fori_loop(0, NB, step, (zero, zero))
        total = lax.dot_general(
            jnp.ones((8, cells), jnp.float32),
            jnp.concatenate([norm, curve], 0),
            (((1,), (1,)), ((), ())),
            precision=HIGHEST,
            preferred_element_type=jnp.float32,
        )
        total = group_sum(total, "ey", turn, 0, pr_ey, sum_send_ey, sum_recv_ey)
        total = group_sum(total, "ex", turn, 1, pr_ex, sum_send_ex, sum_recv_ex)
        row = lax.broadcasted_iota(jnp.int32, (modes, 2 * modes), 0)
        column = lax.broadcasted_iota(jnp.int32, (modes, 2 * modes), 1)
        pick = lambda offset: jnp.sum(
            jnp.where(column == row + offset, total[0:1, :], 0.0), axis=1, keepdims=True
        )
        return pick(0), pick(modes)

    res_ref[...] = cond_ref[...]
    assemble(res_ref, 0)
    for ref in (x_ref, dir_ref, along_ref):
        ref[...] = jnp.zeros_like(ref)

    def sweep(turn, scalars):
        norm_now, step_size = scalars
        operator(turn + 1)
        norm_next, curve_now = paired(turn)
        conj_ratio = jnp.where(turn == 0, 0.0, norm_next / norm_now)
        step_size = norm_next / (curve_now - conj_ratio * norm_next / step_size)

        def update(n, carry):
            rows = node(n)
            search = res_ref[rows, :] + conj_ratio * dir_ref[rows, :]
            along = app_ref[rows, :] + conj_ratio * along_ref[rows, :]
            x_ref[rows, :] = x_ref[rows, :] + step_size * search
            dir_ref[rows, :] = search
            along_ref[rows, :] = along
            res_ref[rows, :] = res_ref[rows, :] - step_size * along
            return carry

        lax.fori_loop(0, NB, update, 0)
        return norm_next, step_size

    one = jnp.ones((modes, 1), jnp.float32)
    lax.fori_loop(0, ITERS, sweep, (one, one))


def conjugate_gradients(condensed, stacked, scaling, keep, weights):
    modes, cells = condensed.shape[1:]
    field = pltpu.VMEM((NB * modes, cells), jnp.float32)
    along_ex, along_ey = lax.axis_size("ex") - 1, lax.axis_size("ey") - 1
    turns = ITERS + 1
    strips = lambda *lead: pltpu.VMEM(lead + (modes, cells), jnp.float32)
    tile = lambda *lead: pltpu.VMEM(lead + (8, 2 * modes), jnp.float32)
    semaphores = lambda *dims: pltpu.SemaphoreType.DMA(dims)
    whole = pl.BlockSpec(memory_space=pltpu.VMEM)
    solved = pl.pallas_call(
        functools.partial(cg_kernel, modes),
        out_shape=jax.ShapeDtypeStruct((NB * modes, cells), jnp.float32),
        in_specs=[whole] * 5,
        out_specs=whole,
        scratch_shapes=[field] * 4
        + [
            strips(turns, 2, 2),
            strips(turns, 2, 2),
            strips(turns, 2),
            strips(turns, 3, 2),
            tile(ITERS, 2),
            tile(ITERS, along_ex),
            tile(ITERS, along_ey),
            semaphores(turns, 8),
            semaphores(turns, 8),
            semaphores(ITERS, along_ex),
            semaphores(ITERS, along_ex),
            semaphores(ITERS, along_ey),
            semaphores(ITERS, along_ey),
        ],
        compiler_params=pltpu.CompilerParams(
            collective_id=0, has_side_effects=True, vmem_limit_bytes=40 << 20
        ),
        cost_estimate=pl.CostEstimate(flops=10**9, bytes_accessed=2 * 10**8, transcendentals=0),
    )(condensed.reshape(NB * modes, cells), stacked, scaling[None], keep, weights)
    return solved.reshape(NB, modes, cells)


def on_device(forcing, element_coef, schur, couple, inner_inv, element_cell):
    modes_dev = schur.shape[0]
    planes_dev = forcing.shape[0]
    elements = forcing.shape[2]
    groups = lax.axis_size("fourier")
    me = lax.axis_index("fourier")
    dft_table = dft_rows(modes_dev * groups)
    swap = [[(i, (i + hop) % groups) for i in range(groups)] for hop in range(groups)]
    plane_of = lambda group: lax.dynamic_slice_in_dim(dft_table, group * planes_dev, planes_dev, 1)
    rows_of = lambda table, group: lax.dynamic_slice_in_dim(table, group * modes_dev, modes_dev, 0)

    own_planes = plane_of(me)
    one_hot = (element_cell[:, None] == jnp.arange(elements)[None, :]).astype(jnp.float32)
    scaling = jnp.einsum("e,ec->c", element_coef, one_hot, precision=HIGHEST)

    order = [(me - hop) % groups for hop in range(groups)]
    middle = couple.shape[1] // 2
    folded = jnp.concatenate([couple[:, :middle], couple[:, middle:]], 0)
    couples = [couple]
    for hop in range(1, groups):
        arrived = lax.ppermute(folded, "fourier", swap[hop])
        couples.append(jnp.concatenate([arrived[:modes_dev], arrived[modes_dev:]], 1))

    partial = []
    condensed = None
    for hop in range(groups):
        spec = jnp.einsum(
            "mz,zne->mne", rows_of(own_planes, order[hop]), forcing, precision=HIGH
        )
        partial.append(spec[:, NB:])
        term = spec[:, :NB] - jnp.einsum("mbi,mie->mbe", couples[hop], spec[:, NB:], precision=HIGH)
        if hop:
            term = lax.ppermute(term, "fourier", [(b, a) for a, b in swap[hop]])
        condensed = term if condensed is None else condensed + term

    half, inner_count = modes_dev // 2, inner_inv.shape[2]
    padded = jnp.pad(inner_inv, ((0, 0), (0, 0), (0, elements // 2 - inner_count)))
    parcel = jnp.concatenate(
        [forcing[:, NB:], jnp.concatenate([padded[:half], padded[half:]], 2)], 0
    )
    keep, weights = node_masks()
    high, low = split_high_low(schur)
    stacked = jnp.concatenate([high, high, low], 2)
    condensed, parcel, stacked, scaling, keep, weights = lax.optimization_barrier(
        (condensed, parcel, stacked, scaling, keep, weights)
    )
    parcels = [None] + [lax.ppermute(parcel, "fourier", swap[h]) for h in range(1, groups)]
    condensed = jnp.einsum("mbe,ec->bmc", condensed, one_hot, precision=HIGH)
    iterate = conjugate_gradients(condensed, stacked, scaling, keep, weights)
    iterate = jnp.einsum("bmc,ec->mbe", iterate, one_hot, precision=HIGH)

    cycles = [iterate] + [lax.ppermute(iterate, "fourier", swap[h]) for h in range(1, groups)]
    bases = []
    for hop in range(groups):
        inverse = inner_inv
        if hop:
            pairs = parcels[hop][planes_dev:]
            inverse = jnp.concatenate(
                [pairs[:, :, :inner_count], pairs[:, :, elements // 2 :][:, :, :inner_count]], 0
            )
        inner = partial[hop]
        for far in range(1, groups):
            inner = inner + jnp.einsum(
                "mz,zne->mne",
                rows_of(plane_of(order[far]), order[hop]),
                parcels[far][:planes_dev],
                precision=HIGH,
            )
        bases.append(jnp.einsum("mij,mje->mie", inverse, inner, precision=HIGH) / element_coef)

    def back(hop, cycle, base):
        interior = base - jnp.einsum("mbi,mbe->mie", couples[hop], cycle, precision=HIGH)
        return jnp.einsum(
            "mz,mne->zne",
            rows_of(own_planes, order[hop]),
            jnp.concatenate([cycle, interior], 1),
            precision=HIGH,
        )

    velocity = back(0, iterate, bases[0])
    velocity, bases, cycles = lax.optimization_barrier((velocity, bases[1:], cycles[1:]))
    for hop in range(1, groups):
        velocity = velocity + back(hop, cycles[hop - 1], bases[hop - 1])
    return velocity


def solution(mesh):
    placed = (
        P("fourier", None, ("ex", "ey")),
        P(("ex", "ey")),
        P("fourier", None, None),
        P("fourier", None, None),
        P("fourier", None, None),
        P(("ex", "ey")),
    )
    return jax.shard_map(
        on_device,
        mesh=mesh,
        in_specs=placed,
        out_specs=P("fourier", None, ("ex", "ey")),
        check_vma=False,
    )
```

profile of v0, /device:TPU:0, one launch (start us, length us, event | category | flops | bytes accessed | tf_op | source)
XLA Modules:
  0.0 141.2 jit_solution(1311485267782795448)
XLA Ops:
  0.0 1.2 fusion.64
  1.2 0.9 pad_maximum_fusion.6
  2.2 3.0 %collective-permute-start = (f32[128,16,49]{0,1,2:T(8,128)}, f32[128,16,49]{0,1,2:T(8,128)}, u32[]{:S(2)}, u32[]{:S(2)}) collective-permute-start(f32[128,16,49]{0,1,2:T(8,128)} %pad_maximum_fusion.6), channel_id=1, source_target_pairs={{0,16},{16,0},{1,17},{17,1},{2,18},{18,2},{3,19},{19,3},{4,20},{20... | collective-permute-start | bytes 1204232 | tf_op jit(solution)/shard_map/ppermute | solution.py:408
  5.3 0.9 copy.54
  6.2 0.9 copy.53
  7.2 0.0 copy-start.16
  7.2 0.0 copy-start.22
  7.2 0.0 copy-start.3
  7.2 1.2 fusion.63
  8.4 0.2 convolution_bitcast_fusion.1
  8.6 0.4 select_select_fusion
  9.0 0.4 copy-done.3
  9.3 1.4 fusion.39
  10.7 5.4 %fusion.41 = f32[64,81,128]{2,0,1:T(8,128)} fusion(f32[64,81,128]{2,0,1:T(8,128)} %param.11, f32[128,128]{1,0:T(8,128)S(1)} %select_select_fusion, s32[]{:T(128)S(6)} %select_n.133, s32[]{:T(128)S(6)} %select_n.135), kind=kOutput, calls=%fused_computation.47 | convolution fusion | flops 254803968 | bytes 5341192 | tf_op jit(solution)/shard_map/mz,zne->mne/dot_general | solution.py:414
  16.2 0.0 collective-permute-done
  16.2 1.4 fusion.65
  17.6 0.4 copy.74
  18.0 0.4 copy.75
  18.4 1.8 %fusion.11 = f32[64,32,128]{2,1,0:T(8,128)S(1)} fusion(f32[64,49,128]{2,0,1:T(8,128)S(1)} %slice-done, f32[64,16,49]{2,1,0:T(8,128)S(1)} %copy.75, f32[64,16,49]{2,1,0:T(8,128)S(1)} %copy.74), kind=kOutput, calls=%fused_computation.14 | convolution fusion | flops 77170688 | bytes 3055616 | tf_op jit(solution)/shard_map/mbi,mie->mbe/dot_general | solution.py:418
  20.2 0.1 copy-done.1
  20.3 1.7 %slice_subtract_fusion = f32[64,32,128]{2,0,1:T(8,128)} fusion(f32[64,81,128]{2,0,1:T(8,128)S(1)} %copy-done.1, f32[64,32,128]{2,1,0:T(8,128)S(1)} %fusion.11), kind=kLoop, calls=%fused_computation.30 | loop fusion | flops 262144 | bytes 3145728 | tf_op jit(solution)/shard_map/sub | solution.py:418
  22.0 0.3 collective-permute-start.1
  22.3 2.0 %copy.46 = f32[64,32,49]{2,1,0:T(8,128)} copy(f32[64,32,49]{0,1,2:T(8,128)S(1)} %copy-done.11) | data formatting | bytes 802816 | tf_op args[3]
  24.3 2.0 %copy.52 = f32[64,49,49]{2,0,1:T(8,128)S(1)} copy(f32[64,49,49]{0,2,1:T(8,128)} %param.15) | data formatting | bytes 1229312 | tf_op args[4]
  26.3 1.5 %pad_maximum_fusion.5.schur_ref = bf16[64,32,96]{2,1,0:T(8,128)(2,1)S(1)} fusion(bf16[64,32,32]{2,1,0:T(8,128)(2,1)} %get-tuple-element.28, bf16[64,32,32]{2,1,0:T(8,128)(2,1)S(1)} %copy-done.13), kind=kLoop, calls=%fused_computation.36 | loop fusion | flops 1179648 | bytes 655360 | tf_op jit(solution)/shard_map/concatenate | solution.py:430
  27.8 0.0 slice-start.1
  27.8 0.2 pad_slice_fusion.1
  28.0 1.2 slice-done.1
  29.2 0.0 copy-start.21
  29.3 0.0 slice-start.2
  29.3 1.9 %maximum_maximum_fusion = f32[96,49,128]{2,0,1:T(8,128)} fusion(f32[32,49,64]{2,0,1:T(8,128)S(1)} %get-tuple-element.26, f32[32,49,64]{2,0,1:T(8,128)S(1)} %get-tuple-element.25, f32[64,49,128]{2,0,1:T(8,128)S(1)} %slice-done.1), kind=kLoop, calls=%fused_computation.6 | loop fusion | flops 1204224 | bytes 4816896 | tf_op jit(solution)/shard_map/concatenate | solution.py:425
  31.2 0.1 broadcast_multiply_fusion
  31.3 0.6 copy-done.9
  31.9 2.0 %fusion.13 = f32[64,128,32]{1,2,0:T(8,128)S(1)} fusion(f32[64,32,49]{2,1,0:T(8,128)S(1)} %copy-done.9, f32[64,49,128]{2,0,1:T(8,128)S(1)} %slice-done.2), kind=kOutput, calls=%fused_computation.16 | convolution fusion | flops 77070336 | bytes 3055616 | tf_op jit(solution)/shard_map/mbi,mie->mbe/dot_general | solution.py:418
  33.9 13.1 %collective-permute-done.1 = f32[64,32,128]{2,0,1:T(8,128)} collective-permute-done((f32[64,32,128]{2,0,1:T(8,128)}, f32[64,32,128]{2,0,1:T(8,128)}, u32[]{:S(2)}, u32[]{:S(2)}) %collective-permute-start.1) | collective-permute-done | bytes 1048608 | tf_op jit(solution)/shard_map/ppermute | solution.py:420
  46.9 3.0 %fusion.30 = f32[64,32,128]{2,0,1:T(8,128)} fusion(f32[64,32,128]{2,0,1:T(8,128)} %collective-permute-done.1, f32[64,81,128]{2,0,1:T(8,128)S(1)} %copy-done.4, f32[64,128,32]{1,2,0:T(8,128)S(1)} %fusion.13), kind=kLoop, calls=%fused_computation.32 | loop fusion | flops 524288 | bytes 4194304 | tf_op jit(solution)/shard_map/add | solution.py:421
  50.0 0.3 collective-permute-start.2
  50.2 3.8 %copy.57 = f32[64,49,49]{2,1,0:T(8,128)} copy(f32[64,49,49]{0,2,1:T(8,128)} %param.15) | data formatting | bytes 1229312 | tf_op args[4]
  54.0 1.7 %fusion.34 = f32[128,64,32]{0,1,2:T(8,128)S(1)} fusion(f32[64,32,128]{2,0,1:T(8,128)} %fusion.30, s32[128]{0:T(128)S(1)} %copy-done.16), kind=kOutput, calls=%fused_computation.40 | convolution fusion | flops 201342976 | bytes 2097664 | tf_op jit(solution)/shard_map/mbe,ec->bmc/dot_general | solution.py:435
  55.8 52.9 %shard_map.109 = f32[2048,128]{1,0:T(8,128)S(1)} custom-call(f32[2048,128]{1,0:T(8,128)S(1)} %bitcast.45, bf16[64,32,96]{2,1,0:T(8,128)(2,1)S(1)} %pad_maximum_fusion.5.schur_ref, f32[1,128]{1,0:T(1,128)S(1)} %bitcast.47, f32[32,128]{1,0:T(8,128)S(1)} %get-tuple-element.17.keep_ref, f32[32,128]{1,0:T(8,128)S(1)} %get-tuple-element.18.weight_ref), custom_call_target="tpu_custom_call" | custom-call | flops 1000000000 | bytes 200000000 | tf_op jit(solution)/shard_map/pallas_call | solution.py:359
  108.7 0.5 convolution_bitcast_fusion
  109.2 0.6 copy.60
  109.8 1.5 %collective-permute-start.3 = (f32[64,32,128]{2,0,1:T(8,128)S(1)}, f32[64,32,128]{2,0,1:T(8,128)S(1)}, u32[]{:S(2)}, u32[]{:S(2)}) collective-permute-start(f32[64,32,128]{2,0,1:T(8,128)S(1)} %convolution_bitcast_fusion), channel_id=1, source_target_pairs={{0,16},{16,0},{1,17},{17,1},{2,18},{18,2},{3,19},{19,3},{4,20},{20... | collective-permute-start | bytes 3145736 | tf_op jit(solution)/shard_map/ppermute | solution.py:439
  111.4 0.3 fusion.62
  111.7 0.0 copy-start.5
  111.7 0.5 copy.76
  112.2 0.5 copy.77
  112.7 0.8 copy-done.5
  113.4 1.0 fusion.19
  114.5 0.5 copy-done.6
  114.9 2.5 %fusion.9 = f32[64,128,49]{1,2,0:T(8,128)S(1)} fusion(f32[64,49,49]{2,1,0:T(8,128)S(1)} %copy-done.6, f32[64,49,128]{2,0,1:T(8,128)S(1)} %fusion.19), kind=kOutput, calls=%fused_computation.12 | convolution fusion | flops 118013952 | bytes 3825920 | tf_op jit(solution)/shard_map/mij,mje->mie/dot_general | solution.py:456
  117.4 2.1 %subtract_bitcast_fusion = f32[64,49,128]{2,1,0:T(8,128)S(1)} fusion(f32[64,128,49]{1,2,0:T(8,128)S(1)} %fusion.9, f32[64,32,49]{2,1,0:T(8,128)S(1)} %copy-done.10, f32[128]{0:T(128)S(1)} %copy-done.22, f32[64,32,128]{2,0,1:T(8,128)S(1)} %convolution_bitcast_fusion), kind=kOutput, calls=%fused_computation.18 | convolution fusion | flops 77873152 | bytes 4661760 | tf_op jit(solution)/shard_map/mbi,mbe->mie/dot_general | solution.py:459
  119.5 0.2 pad_maximum_fusion
  119.7 1.5 %copy-done.2 = f32[64,81,128]{2,0,1:T(8,128)S(1)} copy-done((f32[64,81,128]{2,0,1:T(8,128)S(1)}, f32[64,81,128]{2,0,1:T(8,128)}, u32[]{:S(2)}) %copy-start.2) | copy-done | bytes 2654232
  121.2 0.9 fusion.22
  122.2 1.5 %fusion.2 = f32[64,81,128]{2,0,1:T(8,128)S(1)} fusion(f32[64,81,128]{2,1,0:T(8,128)S(1)} %pad_maximum_fusion, f32[128,128]{1,0:T(8,128)S(1)} %copy-done.15, s32[]{:T(128)S(6)} %select_n.133, s32[]{:T(128)S(6)} %select_n.135), kind=kOutput, calls=%fused_computation.4 | convolution fusion | flops 254803968 | bytes 5570568 | tf_op jit(solution)/shard_map/mz,mne->zne/dot_general | solution.py:460
  123.7 2.6 %fusion.25 = f32[64,49,128]{2,1,0:T(8,128)S(1)} fusion(f32[64,49,128]{2,0,1:T(8,128)S(1)} %fusion.22, f32[32,49,49]{2,1,0:T(8,128)S(1)} %copy.77, f32[32,49,49]{2,1,0:T(8,128)S(1)} %copy.76, f32[128]{0:T(128)S(1)} %copy-done.22), kind=kOutput, calls=%fused_computation.28 | convolution fusion | flops 118569024 | bytes 3826432 | tf_op jit(solution)/shard_map/mij,mje->mie/dot_general | solution.py:456
  126.3 8.2 %collective-permute-done.3 = f32[64,32,128]{2,0,1:T(8,128)S(1)} collective-permute-done((f32[64,32,128]{2,0,1:T(8,128)S(1)}, f32[64,32,128]{2,0,1:T(8,128)S(1)}, u32[]{:S(2)}, u32[]{:S(2)}) %collective-permute-start.3) | collective-permute-done | bytes 1048608 | tf_op jit(solution)/shard_map/ppermute | solution.py:439
  134.6 2.0 %fusion.31 = f32[64,49,128]{2,1,0:T(8,128)S(1)} fusion(f32[64,16,49]{2,1,0:T(8,128)S(1)} %copy-done.8, f32[64,16,49]{2,1,0:T(8,128)S(1)} %copy.74, f32[64,32,128]{2,0,1:T(8,128)S(1)} %collective-permute-done.3), kind=kOutput, calls=%fused_computation.35 | convolution fusion | flops 77170688 | bytes 3055616 | tf_op jit(solution)/shard_map/mbi,mbe->mie/dot_general | solution.py:459
  136.6 0.6 copy.67
  137.2 0.2 sub.47
  137.4 0.2 pad_maximum_fusion.1
  137.6 1.5 %fusion = f32[64,81,128]{2,0,1:T(8,128)S(1)} fusion(f32[64,81,128]{2,1,0:T(8,128)S(1)} %pad_maximum_fusion.1, f32[128,128]{1,0:T(8,128)S(1)} %copy-done.15, s32[]{:T(128)S(6)} %select_n.138, s32[]{:T(128)S(6)} %select_n.135), kind=kOutput, calls=%fused_computation.2 | convolution fusion | flops 254803968 | bytes 5570568 | tf_op jit(solution)/shard_map/mz,mne->zne/dot_general | solution.py:460
  139.1 2.0 %add.148 = f32[64,81,128]{2,0,1:T(8,128)} add(f32[64,81,128]{2,0,1:T(8,128)S(1)} %fusion.2, f32[64,81,128]{2,0,1:T(8,128)S(1)} %fusion) | non-fusion elementwise | flops 663552 | bytes 7962624 | tf_op jit(solution)/shard_map/add | solution.py:470
  (45 shorter events, 0.2 us)
Async XLA Ops:
  0.0 5.2 %copy-start.12 = (f32[64,32,32]{0,2,1:T(8,128)S(1)}, f32[64,32,32]{0,2,1:T(8,128)}, u32[]{:S(2)}) copy-start(f32[64,32,32]{0,2,1:T(8,128)} %param.13) | copy-start | bytes 786436
  2.2 14.0 %collective-permute-start = (f32[128,16,49]{0,1,2:T(8,128)}, f32[128,16,49]{0,1,2:T(8,128)}, u32[]{:S(2)}, u32[]{:S(2)}) collective-permute-start(f32[128,16,49]{0,1,2:T(8,128)} %pad_maximum_fusion.6), channel_id=1, source_target_pairs={{0,16},{16,0},{1,17},{17,1},{2,18},{18,2},{3,19},{19,3},{4,20},{20... | collective-permute-start | bytes 1204232 | tf_op jit(solution)/shard_map/ppermute | solution.py:408
  7.2 1.3 copy-start.16
  7.2 1.2 copy-start.22
  7.2 2.1 %copy-start.3 = (f32[64,81,128]{2,0,1:T(8,128)S(1)}, f32[64,81,128]{2,0,1:T(8,128)}, u32[]{:S(2)}) copy-start(f32[64,81,128]{2,0,1:T(8,128)} %param.11) | copy-start | bytes 7962628
  9.3 1.4 %copy-start.14 = (f32[128,128]{1,0:T(8,128)}, f32[128,128]{1,0:T(8,128)S(1)}, u32[]{:S(2)}) copy-start(f32[128,128]{1,0:T(8,128)S(1)} %select_select_fusion) | copy-start | bytes 196612
  10.7 5.5 %copy-start = (f32[64,81,128]{2,0,1:T(8,128)}, f32[64,81,128]{2,0,1:T(8,128)S(1)}, u32[]{:S(2)}) copy-start(f32[64,81,128]{2,0,1:T(8,128)S(1)} %fusion.39) | copy-start | bytes 7962628
  16.2 2.2 %slice-start = ((f32[64,81,128]{2,0,1:T(8,128)}), f32[64,49,128]{2,0,1:T(8,128)S(1)}, s32[]{:S(2)}) async-start(f32[64,81,128]{2,0,1:T(8,128)} %copy-done), calls=%async_computation | async-start | bytes 3211264 | tf_op jit(solution)/shard_map/slice | solution.py:418
  18.4 1.8 %copy-start.7 = (f32[64,16,49]{2,1,0:T(8,128)}, f32[64,16,49]{2,1,0:T(8,128)S(1)}, u32[]{:S(2)}) copy-start(f32[64,16,49]{2,1,0:T(8,128)S(1)} %copy.75) | copy-start | bytes 602116
  18.4 1.9 %copy-start.1 = (f32[64,81,128]{2,0,1:T(8,128)S(1)}, f32[64,81,128]{2,0,1:T(8,128)}, u32[]{:S(2)}) copy-start(f32[64,81,128]{2,0,1:T(8,128)} %copy-done) | copy-start | bytes 7962628
  20.3 2.0 %copy-start.11 = (f32[64,32,49]{0,1,2:T(8,128)S(1)}, f32[64,32,49]{0,1,2:T(8,128)}, u32[]{:S(2)}) copy-start(f32[64,32,49]{0,1,2:T(8,128)} %param.14) | copy-start | bytes 1204228
  22.0 24.9 %collective-permute-start.1 = (f32[64,32,128]{2,0,1:T(8,128)}, f32[64,32,128]{2,0,1:T(8,128)}, u32[]{:S(2)}, u32[]{:S(2)}) collective-permute-start(f32[64,32,128]{2,0,1:T(8,128)} %slice_subtract_fusion), channel_id=1, source_target_pairs={{16,0},{0,16},{17,1},{1,17},{18,2},{2,18},{19,3},{3,19},{20,4},{4,... | collective-permute-start | bytes 3145736 | tf_op jit(solution)/shard_map/ppermute | solution.py:420
  24.3 2.0 %copy-start.13 = (bf16[64,32,32]{2,1,0:T(8,128)(2,1)S(1)}, bf16[64,32,32]{2,1,0:T(8,128)(2,1)}, u32[]{:S(2)}) copy-start(bf16[64,32,32]{2,1,0:T(8,128)(2,1)} %get-tuple-element.27) | copy-start | bytes 393220
  27.8 1.4 %slice-start.1 = ((f32[64,81,128]{2,0,1:T(8,128)}), f32[64,49,128]{2,0,1:T(8,128)S(1)}, s32[]{:S(2)}) async-start(f32[64,81,128]{2,0,1:T(8,128)} %param.11), calls=%async_computation.1 | async-start | bytes 3211264 | tf_op jit(solution)/shard_map/slice | solution.py:426
  29.2 2.0 %copy-start.17 = (pred[32]{0:T(512)(128)(4,1)S(1)}, pred[32]{0:T(512)(128)(4,1)}, u32[]{:S(2)}) copy-start(pred[32]{0:T(512)(128)(4,1)} %constant.173) | copy-start | bytes 100
  29.2 2.0 %copy-start.18 = (pred[32]{0:T(512)(128)(4,1)S(1)}, pred[32]{0:T(512)(128)(4,1)}, u32[]{:S(2)}) copy-start(pred[32]{0:T(512)(128)(4,1)} %constant.174) | copy-start | bytes 100
  29.2 2.0 %copy-start.19 = (pred[32]{0:T(512)(128)(4,1)S(1)}, pred[32]{0:T(512)(128)(4,1)}, u32[]{:S(2)}) copy-start(pred[32]{0:T(512)(128)(4,1)} %constant.175) | copy-start | bytes 100
  29.2 2.0 %copy-start.20 = (pred[32]{0:T(512)(128)(4,1)S(1)}, pred[32]{0:T(512)(128)(4,1)}, u32[]{:S(2)}) copy-start(pred[32]{0:T(512)(128)(4,1)} %constant.176) | copy-start | bytes 100
  29.2 2.0 %copy-start.21 = (f32[32]{0:T(128)S(1)}, f32[32]{0:T(128)}, u32[]{:S(2)}) copy-start(f32[32]{0:T(128)} %constant.177) | copy-start | bytes 388
  29.3 2.0 %slice-start.2 = ((f32[64,81,128]{2,0,1:T(8,128)}), f32[64,49,128]{2,0,1:T(8,128)S(1)}, s32[]{:S(2)}) async-start(f32[64,81,128]{2,0,1:T(8,128)} %fusion.41), calls=%async_computation.2 | async-start | bytes 3211264 | tf_op jit(solution)/shard_map/slice | solution.py:418
  29.3 2.6 %copy-start.9 = (f32[64,32,49]{2,1,0:T(8,128)S(1)}, f32[64,32,49]{2,1,0:T(8,128)}, u32[]{:S(2)}) copy-start(f32[64,32,49]{2,1,0:T(8,128)} %copy.46) | copy-start | bytes 1204228
  31.9 15.0 %copy-start.4 = (f32[64,81,128]{2,0,1:T(8,128)S(1)}, f32[64,81,128]{2,0,1:T(8,128)}, u32[]{:S(2)}) copy-start(f32[64,81,128]{2,0,1:T(8,128)} %fusion.41) | copy-start | bytes 7962628
  50.0 61.4 %collective-permute-start.2 = (f32[96,49,128]{2,0,1:T(8,128)}, f32[96,49,128]{2,0,1:T(8,128)S(1)}, u32[]{:S(2)}, u32[]{:S(2)}) collective-permute-start(f32[96,49,128]{2,0,1:T(8,128)} %maximum_maximum_fusion), channel_id=1, source_target_pairs={{0,16},{16,0},{1,17},{17,1},{2,18},{18,2},{3,19},{19,3},{4,20},{20... | collective-permute-start | bytes 7225352 | tf_op jit(solution)/shard_map/ppermute | solution.py:434
  109.8 24.7 %collective-permute-start.3 = (f32[64,32,128]{2,0,1:T(8,128)S(1)}, f32[64,32,128]{2,0,1:T(8,128)S(1)}, u32[]{:S(2)}, u32[]{:S(2)}) collective-permute-start(f32[64,32,128]{2,0,1:T(8,128)S(1)} %convolution_bitcast_fusion), channel_id=1, source_target_pairs={{0,16},{16,0},{1,17},{17,1},{2,18},{18,2},{3,19},{19,3},{4,20},{20... | collective-permute-start | bytes 3145736 | tf_op jit(solution)/shard_map/ppermute | solution.py:439
  111.7 1.8 %copy-start.5 = (f32[64,81,128]{2,0,1:T(8,128)S(1)}, f32[64,81,128]{2,0,1:T(8,128)}, u32[]{:S(2)}) copy-start(f32[64,81,128]{2,0,1:T(8,128)} %fusion.41) | copy-start | bytes 7962628
  111.7 1.7 %copy-start.15 = (f32[128,128]{1,0:T(8,128)S(1)}, f32[128,128]{1,0:T(8,128)}, u32[]{:S(2)}) copy-start(f32[128,128]{1,0:T(8,128)} %copy-done.14) | copy-start | bytes 196612
  113.4 1.5 %copy-start.6 = (f32[64,49,49]{2,1,0:T(8,128)S(1)}, f32[64,49,49]{2,1,0:T(8,128)}, u32[]{:S(2)}) copy-start(f32[64,49,49]{2,1,0:T(8,128)} %copy.57) | copy-start | bytes 1843972
  114.9 2.5 %copy-start.10 = (f32[64,32,49]{2,1,0:T(8,128)S(1)}, f32[64,32,49]{2,1,0:T(8,128)}, u32[]{:S(2)}) copy-start(f32[64,32,49]{2,1,0:T(8,128)} %copy.46) | copy-start | bytes 1204228
  119.5 1.8 %copy-start.2 = (f32[64,81,128]{2,0,1:T(8,128)S(1)}, f32[64,81,128]{2,0,1:T(8,128)}, u32[]{:S(2)}) copy-start(f32[64,81,128]{2,0,1:T(8,128)} %copy-done) | copy-start | bytes 7962628
  123.7 10.9 %copy-start.8 = (f32[64,16,49]{2,1,0:T(8,128)S(1)}, f32[64,16,49]{2,1,0:T(8,128)}, u32[]{:S(2)}) copy-start(f32[64,16,49]{2,1,0:T(8,128)} %copy-done.7) | copy-start | bytes 602116
where the time goes:
time: 142 us; the launch traced here: 141 us
  Pallas kernels  52.9 us (37%)
  matrix products  27.1 us (19%)
  waiting for transfers between devices  21.3 us (15%)
  local copies, waits for them, and re-layouts  20.8 us (15%)
  other arithmetic  13.5 us (10%)
  starting transfers between devices  5.1 us (4%)
    pallas_call x1, Pallas kernels, conjugate_gradients(): pl.pallas_call(functools.partial(cg_kernel, modes), out_shape=jax.ShapeDt...  52.9 us
    unnamed x54, local copies, waits for them, and re-layouts  14.3 us
    ppermute x1, waiting for transfers between devices, on_device(): term = lax.ppermute(term, 'fourier', [(b, a) for a, b in swap[hop]])  13.1 us
    ppermute x1, waiting for transfers between devices, on_device(): lax.ppermute(iterate, 'fourier', swap[h])  8.21 us
    dot_general x2, matrix products, on_device(): jnp.einsum('mz,zne->mne', rows_of(own_planes, order[hop]), forcing, preci...  6.79 us
    dot_general x2, matrix products, on_device(): jnp.einsum('mij,mje->mie', inverse, inner, precision=HIGH) / element_coef  5.11 us
    dot_general x2, matrix products, back(): jnp.einsum('mbi,mbe->mie', couples[hop], cycle, precision=HIGH)  4.08 us
    dot_general x2, matrix products, on_device(): jnp.einsum('mbi,mie->mbe', couples[hop], spec[:, NB:], precision=HIGH)  3.75 us
  transfers between devices with their start and end apart: 4, of which 2 were waited for; matrix products, arithmetic and copies ran while one was open for 27% of the time, Pallas kernels for 37%

commit v1 on v0

--- a/solution.py
+++ b/solution.py
@@ -435,6 +435,7 @@
     condensed = jnp.einsum("mbe,ec->bmc", condensed, one_hot, precision=HIGH)
     iterate = conjugate_gradients(condensed, stacked, scaling, keep, weights)
     iterate = jnp.einsum("bmc,ec->mbe", iterate, one_hot, precision=HIGH)
+    iterate, inner_inv = lax.optimization_barrier((iterate, inner_inv))
 
     cycles = [iterate] + [lax.ppermute(iterate, "fourier", swap[h]) for h in range(1, groups)]
     bases = []

time: 142 us -> 140 us (0.986)
  waiting for transfers between devices: 21.3 us -> 16.3 us
  local copies, waits for them, and re-layouts: 20.8 us -> 23.4 us
  matrix products: 27.1 us -> 29.3 us
    optimization_barrier x0 -> x2, local copies, waits for them, and re-layouts: none -> 6.57 us  [on_device(): iterate, inner_inv = lax.optimization_barrier((iterate, inner_inv))]
    ppermute x1, waiting for transfers between devices: 8.21 us -> 3.75 us  [on_device(): lax.ppermute(iterate, 'fourier', swap[h])]
    unnamed x54 -> x59, local copies, waits for them, and re-layouts: 14.3 us -> 10.5 us
    dot_general x2, matrix products: 4.08 us -> 6.8 us  [back(): jnp.einsum('mbi,mbe->mie', couples[hop], cycle, precision=HIGH)]
  transfers between devices with their start and end apart: 4 -> 4, of which waited for: 2 -> 2; matrix products, arithmetic and copies ran while one was open for 27% -> 29% of each run, Pallas kernels for 37% -> 38%
where the time goes in v1:
time: 140 us
  Pallas kernels  52.9 us (38%)
  matrix products  29.3 us (21%)
  local copies, waits for them, and re-layouts  23.4 us (17%)
  waiting for transfers between devices  16.3 us (12%)
  other arithmetic  12.4 us (9%)
  starting transfers between devices  4.94 us (4%)
    pallas_call x1, Pallas kernels, conjugate_gradients(): pl.pallas_call(functools.partial(cg_kernel, modes), out_shape=jax.ShapeDt...  52.9 us
    ppermute x1, waiting for transfers between devices, on_device(): term = lax.ppermute(term, 'fourier', [(b, a) for a, b in swap[hop]])  12.5 us
    unnamed x59, local copies, waits for them, and re-layouts  10.5 us
    dot_general x2, matrix products, back(): jnp.einsum('mbi,mbe->mie', couples[hop], cycle, precision=HIGH)  6.8 us
    dot_general x2, matrix products, on_device(): jnp.einsum('mz,zne->mne', rows_of(own_planes, order[hop]), forcing, preci...  6.79 us
    optimization_barrier x2, local copies, waits for them, and re-layouts, on_device(): iterate, inner_inv = lax.optimization_barrier((iterate, inner_inv))  6.57 us
    dot_general x2, matrix products, on_device(): jnp.einsum('mij,mje->mie', inverse, inner, precision=HIGH) / element_coef  4.8 us
    ppermute x1, waiting for transfers between devices, on_device(): lax.ppermute(iterate, 'fourier', swap[h])  3.75 us
  transfers between devices with their start and end apart: 4, of which 2 were waited for; matrix products, arithmetic and copies ran while one was open for 29% of the time, Pallas kernels for 38%

profile of v1, /device:TPU:0, one launch (start us, length us, event | category | flops | bytes accessed | tf_op | source)
XLA Modules:
  0.0 139.8 jit_solution(10993880417799901281)
XLA Ops:
  0.0 1.2 fusion.64
  1.2 0.2 pad_maximum_fusion.6
  1.4 3.0 %collective-permute-start = (f32[128,16,49]{0,1,2:T(8,128)S(1)}, f32[128,16,49]{0,1,2:T(8,128)S(1)}, u32[]{:S(2)}, u32[]{:S(2)}) collective-permute-start(f32[128,16,49]{0,1,2:T(8,128)S(1)} %pad_maximum_fusion.6), channel_id=1, source_target_pairs={{0,16},{16,0},{1,17},{17,1},{2,18},{18,2},{3,19},{19,3},{4,20},{20... | collective-permute-start | bytes 1204232 | tf_op jit(solution)/shard_map/ppermute | solution.py:408
  4.6 0.9 copy.52
  5.5 0.9 copy.51
  6.5 0.0 copy-start.3
  6.5 1.2 fusion.63
  7.7 0.2 convolution_bitcast_fusion.1
  7.9 0.4 select_select_fusion
  8.3 0.4 copy-done.3
  8.6 1.4 fusion.39
  10.1 5.4 %fusion.41 = f32[64,81,128]{2,0,1:T(8,128)} fusion(f32[64,81,128]{2,0,1:T(8,128)} %param.11, f32[128,128]{1,0:T(8,128)S(1)} %select_select_fusion, s32[]{:T(128)S(6)} %select_n.133, s32[]{:T(128)S(6)} %select_n.135), kind=kOutput, calls=%fused_computation.47 | convolution fusion | flops 254803968 | bytes 5341192 | tf_op jit(solution)/shard_map/mz,zne->mne/dot_general | solution.py:414
  15.5 0.2 fusion.65
  15.7 0.4 copy.72
  16.1 0.4 copy.73
  16.4 0.5 slice-done
  16.9 1.8 %fusion.11 = f32[64,32,128]{2,1,0:T(8,128)S(1)} fusion(f32[64,49,128]{2,0,1:T(8,128)S(1)} %slice-done, f32[64,16,49]{2,1,0:T(8,128)S(1)} %copy.73, f32[64,16,49]{2,1,0:T(8,128)S(1)} %copy.72), kind=kOutput, calls=%fused_computation.15 | convolution fusion | flops 77170688 | bytes 3055616 | tf_op jit(solution)/shard_map/mbi,mie->mbe/dot_general | solution.py:418
  18.7 0.1 copy-done.1
  18.9 1.6 %slice_subtract_fusion = f32[64,32,128]{2,0,1:T(8,128)} fusion(f32[64,81,128]{2,0,1:T(8,128)S(1)} %copy-done.1, f32[64,32,128]{2,1,0:T(8,128)S(1)} %fusion.11), kind=kLoop, calls=%fused_computation.30 | loop fusion | flops 262144 | bytes 3145728 | tf_op jit(solution)/shard_map/sub | solution.py:418
  20.5 0.0 collective-permute-start.1
  20.5 0.6 broadcast_compare_fusion
  21.1 2.0 %copy.44 = f32[64,32,49]{2,1,0:T(8,128)} copy(f32[64,32,49]{0,1,2:T(8,128)S(1)} %copy-done.13) | data formatting | bytes 802816 | tf_op args[3]
  23.1 1.3 copy-done.7
  24.5 0.6 copy.50
  25.0 1.8 %pad_maximum_fusion.5.schur_ref = bf16[64,32,96]{2,1,0:T(8,128)(2,1)S(1)} fusion(bf16[64,32,32]{2,1,0:T(8,128)(2,1)} %get-tuple-element.32, bf16[64,32,32]{2,1,0:T(8,128)(2,1)} %get-tuple-element.31), kind=kLoop, calls=%fused_computation.36 | loop fusion | flops 1179648 | bytes 655360 | tf_op jit(solution)/shard_map/concatenate | solution.py:430
  26.9 0.0 slice-start.1
  26.9 0.2 pad_slice_fusion.1
  27.1 1.2 slice-done.1
  28.3 0.0 copy-start.22
  28.3 0.0 slice-start.2
  28.3 1.9 %maximum_maximum_fusion = f32[96,49,128]{2,0,1:T(8,128)} fusion(f32[32,49,64]{2,0,1:T(8,128)S(1)} %get-tuple-element.30, f32[32,49,64]{2,0,1:T(8,128)S(1)} %get-tuple-element.29, f32[64,49,128]{2,0,1:T(8,128)S(1)} %slice-done.1), kind=kLoop, calls=%fused_computation.6 | loop fusion | flops 1204224 | bytes 4816896 | tf_op jit(solution)/shard_map/concatenate | solution.py:425
  30.3 0.1 broadcast_multiply_fusion
  30.4 0.6 copy-done.10
  31.0 2.0 %fusion.13 = f32[64,128,32]{1,2,0:T(8,128)S(1)} fusion(f32[64,32,49]{2,1,0:T(8,128)S(1)} %copy-done.10, f32[64,49,128]{2,0,1:T(8,128)S(1)} %slice-done.2), kind=kOutput, calls=%fused_computation.17 | convolution fusion | flops 77070336 | bytes 3055616 | tf_op jit(solution)/shard_map/mbi,mie->mbe/dot_general | solution.py:418
  32.9 12.5 %collective-permute-done.1 = f32[64,32,128]{2,0,1:T(8,128)} collective-permute-done((f32[64,32,128]{2,0,1:T(8,128)}, f32[64,32,128]{2,0,1:T(8,128)}, u32[]{:S(2)}, u32[]{:S(2)}) %collective-permute-start.1) | collective-permute-done | bytes 1048608 | tf_op jit(solution)/shard_map/ppermute | solution.py:420
  45.4 2.0 %fusion.30 = f32[64,32,128]{2,0,1:T(8,128)S(1)} fusion(f32[64,32,128]{2,0,1:T(8,128)} %collective-permute-done.1, f32[64,81,128]{2,0,1:T(8,128)S(1)} %copy-done.4, f32[64,128,32]{1,2,0:T(8,128)S(1)} %fusion.13), kind=kLoop, calls=%fused_computation.32 | loop fusion | flops 524288 | bytes 4194304 | tf_op jit(solution)/shard_map/add | solution.py:421
  47.4 0.4 collective-permute-start.2
  47.8 0.5 fusion.34
  48.3 52.9 %shard_map.109 = f32[2048,128]{1,0:T(8,128)S(1)} custom-call(f32[2048,128]{1,0:T(8,128)S(1)} %bitcast.45, bf16[64,32,96]{2,1,0:T(8,128)(2,1)S(1)} %pad_maximum_fusion.5.schur_ref, f32[1,128]{1,0:T(1,128)S(1)} %bitcast.47, f32[32,128]{1,0:T(8,128)S(1)} %get-tuple-element.19.keep_ref, f32[32,128]{1,0:T(8,128)S(1)} %get-tuple-element.20.weight_ref), custom_call_target="tpu_custom_call" | custom-call | flops 1000000000 | bytes 200000000 | tf_op jit(solution)/shard_map/pallas_call | solution.py:359
  101.2 1.6 %convolution_bitcast_fusion = f32[64,32,128]{2,0,1:T(8,128)} fusion(f32[32,64,128]{2,1,0:T(8,128)S(1)} %bitcast.46, s32[128]{0:T(128)S(1)} %copy-done.17), kind=kOutput, calls=%fused_computation.27 | convolution fusion | flops 201342976 | bytes 2097664 | tf_op jit(solution)/shard_map/bmc,ec->mbe/dot_general | solution.py:437
  102.7 2.8 %copy.58 = f32[64,32,128]{2,1,0:T(8,128)} copy(f32[64,32,128]{2,0,1:T(8,128)} %convolution_bitcast_fusion) | data formatting | bytes 2097152 | tf_op jit(solution)/shard_map/optimization_barrier | solution.py:438
  105.6 1.5 %collective-permute-start.3 = (f32[64,32,128]{2,0,1:T(8,128)}, f32[64,32,128]{2,0,1:T(8,128)}, u32[]{:S(2)}, u32[]{:S(2)}) collective-permute-start(f32[64,32,128]{2,0,1:T(8,128)} %convolution_bitcast_fusion), channel_id=1, source_target_pairs={{0,16},{16,0},{1,17},{17,1},{2,18},{18,2},{3,19},{19,3},{4,20},{20... | collective-permute-start | bytes 3145736 | tf_op jit(solution)/shard_map/ppermute | solution.py:440
  107.0 3.8 %copy.54 = f32[64,49,49]{2,1,0:T(8,128)} copy(f32[64,49,49]{0,2,1:T(8,128)} %param.15) | data formatting | bytes 1229312 | tf_op jit(solution)/shard_map/optimization_barrier | solution.py:438
  110.8 0.3 fusion.62
  111.1 0.0 copy-start.5
  111.1 0.5 copy.74
  111.6 0.5 copy.75
  112.1 0.8 copy-done.5
  112.9 1.0 fusion.19
  113.9 0.5 copy-done.6
  114.4 2.4 %fusion.9 = f32[64,49,128]{2,1,0:T(8,128)S(1)} fusion(f32[64,49,49]{2,1,0:T(8,128)S(1)} %copy-done.6, f32[64,49,128]{2,0,1:T(8,128)S(1)} %fusion.19), kind=kOutput, calls=%fused_computation.13 | convolution fusion | flops 118013952 | bytes 3825920 | tf_op jit(solution)/shard_map/mij,mje->mie/dot_general | solution.py:457
  116.8 3.3 %bitcast_subtract_fusion = f32[64,49,128]{2,1,0:T(8,128)S(1)} fusion(f32[64,49,128]{2,1,0:T(8,128)S(1)} %fusion.9, f32[64,32,49]{2,1,0:T(8,128)S(1)} %copy-done.11, f32[128]{0:T(128)S(1)} %copy-done.25, f32[64,32,128]{2,0,1:T(8,128)} %convolution_bitcast_fusion), kind=kOutput, calls=%fused_computation.11 | convolution fusion | flops 77873152 | bytes 4661760 | tf_op jit(solution)/shard_map/mbi,mbe->mie/dot_general | solution.py:460
  120.2 0.2 pad_maximum_fusion
  120.4 1.5 %copy-done.2 = f32[64,81,128]{2,0,1:T(8,128)S(1)} copy-done((f32[64,81,128]{2,0,1:T(8,128)S(1)}, f32[64,81,128]{2,0,1:T(8,128)}, u32[]{:S(2)}) %copy-start.2) | copy-done | bytes 2654232
  121.9 0.9 fusion.22
  122.8 1.5 %fusion.2 = f32[64,81,128]{2,0,1:T(8,128)S(1)} fusion(f32[64,81,128]{2,1,0:T(8,128)S(1)} %pad_maximum_fusion, f32[128,128]{1,0:T(8,128)S(1)} %copy-done.16, s32[]{:T(128)S(6)} %select_n.133, s32[]{:T(128)S(6)} %select_n.135), kind=kOutput, calls=%fused_computation.4 | convolution fusion | flops 254803968 | bytes 5570568 | tf_op jit(solution)/shard_map/mz,mne->zne/dot_general | solution.py:461
  124.4 2.4 %fusion.25 = f32[64,49,128]{2,1,0:T(8,128)S(1)} fusion(f32[64,49,128]{2,0,1:T(8,128)S(1)} %fusion.22, f32[32,49,49]{2,1,0:T(8,128)S(1)} %copy.75, f32[32,49,49]{2,1,0:T(8,128)S(1)} %copy.74, f32[128]{0:T(128)S(1)} %copy-done.25), kind=kOutput, calls=%fused_computation.28 | convolution fusion | flops 118569024 | bytes 3826432 | tf_op jit(solution)/shard_map/mij,mje->mie/dot_general | solution.py:457
  126.8 3.8 %collective-permute-done.3 = f32[64,32,128]{2,0,1:T(8,128)} collective-permute-done((f32[64,32,128]{2,0,1:T(8,128)}, f32[64,32,128]{2,0,1:T(8,128)}, u32[]{:S(2)}, u32[]{:S(2)}) %collective-permute-start.3) | collective-permute-done | bytes 1048608 | tf_op jit(solution)/shard_map/ppermute | solution.py:440
  130.5 3.5 %fusion.31 = f32[64,49,128]{2,1,0:T(8,128)S(1)} fusion(f32[64,16,49]{2,1,0:T(8,128)S(1)} %copy-done.9, f32[64,16,49]{2,1,0:T(8,128)S(1)} %copy.72, f32[64,32,128]{2,0,1:T(8,128)} %collective-permute-done.3), kind=kOutput, calls=%fused_computation.35 | convolution fusion | flops 77170688 | bytes 3055616 | tf_op jit(solution)/shard_map/mbi,mbe->mie/dot_general | solution.py:460
  134.0 1.8 %copy.65 = f32[64,32,128]{2,1,0:T(8,128)S(1)} copy(f32[64,32,128]{2,0,1:T(8,128)} %collective-permute-done.3) | data formatting | bytes 2097152 | tf_op jit(solution)/shard_map/optimization_barrier | solution.py:469
  135.8 0.2 sub.43
  136.0 0.2 pad_maximum_fusion.1
  136.2 1.5 %fusion = f32[64,81,128]{2,0,1:T(8,128)S(1)} fusion(f32[64,81,128]{2,1,0:T(8,128)S(1)} %pad_maximum_fusion.1, f32[128,128]{1,0:T(8,128)S(1)} %copy-done.16, s32[]{:T(128)S(6)} %select_n.138, s32[]{:T(128)S(6)} %select_n.135), kind=kOutput, calls=%fused_computation.2 | convolution fusion | flops 254803968 | bytes 5570568 | tf_op jit(solution)/shard_map/mz,mne->zne/dot_general | solution.py:461
  137.7 2.0 %add.148 = f32[64,81,128]{2,0,1:T(8,128)} add(f32[64,81,128]{2,0,1:T(8,128)S(1)} %fusion.2, f32[64,81,128]{2,0,1:T(8,128)S(1)} %fusion) | non-fusion elementwise | flops 663552 | bytes 7962624 | tf_op jit(solution)/shard_map/add | solution.py:471
  (51 shorter events, 0.2 us)
Async XLA Ops:
  0.0 4.5 %copy-start.14 = (f32[64,32,32]{0,2,1:T(8,128)S(1)}, f32[64,32,32]{0,2,1:T(8,128)}, u32[]{:S(2)}) copy-start(f32[64,32,32]{0,2,1:T(8,128)} %param.13) | copy-start | bytes 786436
  1.4 14.1 %collective-permute-start = (f32[128,16,49]{0,1,2:T(8,128)S(1)}, f32[128,16,49]{0,1,2:T(8,128)S(1)}, u32[]{:S(2)}, u32[]{:S(2)}) collective-permute-start(f32[128,16,49]{0,1,2:T(8,128)S(1)} %pad_maximum_fusion.6), channel_id=1, source_target_pairs={{0,16},{16,0},{1,17},{17,1},{2,18},{18,2},{3,19},{19,3},{4,20},{20... | collective-permute-start | bytes 1204232 | tf_op jit(solution)/shard_map/ppermute | solution.py:408
  6.5 1.3 copy-start.17
  6.5 1.2 copy-start.24
  6.5 2.1 %copy-start.3 = (f32[64,81,128]{2,0,1:T(8,128)S(1)}, f32[64,81,128]{2,0,1:T(8,128)}, u32[]{:S(2)}) copy-start(f32[64,81,128]{2,0,1:T(8,128)} %param.11) | copy-start | bytes 7962628
  8.6 1.4 %copy-start.15 = (f32[128,128]{1,0:T(8,128)}, f32[128,128]{1,0:T(8,128)S(1)}, u32[]{:S(2)}) copy-start(f32[128,128]{1,0:T(8,128)S(1)} %select_select_fusion) | copy-start | bytes 196612
  10.0 5.5 %copy-start = (f32[64,81,128]{2,0,1:T(8,128)}, f32[64,81,128]{2,0,1:T(8,128)S(1)}, u32[]{:S(2)}) copy-start(f32[64,81,128]{2,0,1:T(8,128)S(1)} %fusion.39) | copy-start | bytes 7962628
  15.5 1.4 %slice-start = ((f32[64,81,128]{2,0,1:T(8,128)}), f32[64,49,128]{2,0,1:T(8,128)S(1)}, s32[]{:S(2)}) async-start(f32[64,81,128]{2,0,1:T(8,128)} %copy-done), calls=%async_computation | async-start | bytes 3211264 | tf_op jit(solution)/shard_map/slice | solution.py:418
  16.9 1.8 %copy-start.8 = (f32[64,16,49]{2,1,0:T(8,128)}, f32[64,16,49]{2,1,0:T(8,128)S(1)}, u32[]{:S(2)}) copy-start(f32[64,16,49]{2,1,0:T(8,128)S(1)} %copy.73) | copy-start | bytes 602116
  16.9 1.9 %copy-start.1 = (f32[64,81,128]{2,0,1:T(8,128)S(1)}, f32[64,81,128]{2,0,1:T(8,128)}, u32[]{:S(2)}) copy-start(f32[64,81,128]{2,0,1:T(8,128)} %copy-done) | copy-start | bytes 7962628
  18.9 2.2 %copy-start.13 = (f32[64,32,49]{0,1,2:T(8,128)S(1)}, f32[64,32,49]{0,1,2:T(8,128)}, u32[]{:S(2)}) copy-start(f32[64,32,49]{0,1,2:T(8,128)} %param.14) | copy-start | bytes 1204228
  20.5 24.9 %collective-permute-start.1 = (f32[64,32,128]{2,0,1:T(8,128)}, f32[64,32,128]{2,0,1:T(8,128)}, u32[]{:S(2)}, u32[]{:S(2)}) collective-permute-start(f32[64,32,128]{2,0,1:T(8,128)} %slice_subtract_fusion), channel_id=1, source_target_pairs={{16,0},{0,16},{17,1},{1,17},{18,2},{2,18},{19,3},{3,19},{20,4},{4,... | collective-permute-start | bytes 3145736 | tf_op jit(solution)/shard_map/ppermute | solution.py:420
  23.1 1.3 copy-start.7
  26.9 1.4 %slice-start.1 = ((f32[64,81,128]{2,0,1:T(8,128)}), f32[64,49,128]{2,0,1:T(8,128)S(1)}, s32[]{:S(2)}) async-start(f32[64,81,128]{2,0,1:T(8,128)} %param.11), calls=%async_computation.1 | async-start | bytes 3211264 | tf_op jit(solution)/shard_map/slice | solution.py:426
  28.3 1.9 %copy-start.18 = (pred[32]{0:T(512)(128)(4,1)S(1)}, pred[32]{0:T(512)(128)(4,1)}, u32[]{:S(2)}) copy-start(pred[32]{0:T(512)(128)(4,1)} %constant.173) | copy-start | bytes 100
  28.3 1.9 %copy-start.19 = (pred[32]{0:T(512)(128)(4,1)S(1)}, pred[32]{0:T(512)(128)(4,1)}, u32[]{:S(2)}) copy-start(pred[32]{0:T(512)(128)(4,1)} %constant.174) | copy-start | bytes 100
  28.3 1.9 %copy-start.20 = (pred[32]{0:T(512)(128)(4,1)S(1)}, pred[32]{0:T(512)(128)(4,1)}, u32[]{:S(2)}) copy-start(pred[32]{0:T(512)(128)(4,1)} %constant.175) | copy-start | bytes 100
  28.3 1.9 %copy-start.21 = (pred[32]{0:T(512)(128)(4,1)S(1)}, pred[32]{0:T(512)(128)(4,1)}, u32[]{:S(2)}) copy-start(pred[32]{0:T(512)(128)(4,1)} %constant.176) | copy-start | bytes 100
  28.3 1.9 %copy-start.22 = (f32[32]{0:T(128)S(1)}, f32[32]{0:T(128)}, u32[]{:S(2)}) copy-start(f32[32]{0:T(128)} %constant.177) | copy-start | bytes 388
  28.3 1.9 %copy-start.23 = (pred[128]{0:T(512)(128)(4,1)S(1)}, pred[128]{0:T(512)(128)(4,1)}, u32[]{:S(2)}) copy-start(pred[128]{0:T(512)(128)(4,1)} %get-tuple-element.44) | copy-start | bytes 388
  28.3 2.0 %slice-start.2 = ((f32[64,81,128]{2,0,1:T(8,128)}), f32[64,49,128]{2,0,1:T(8,128)S(1)}, s32[]{:S(2)}) async-start(f32[64,81,128]{2,0,1:T(8,128)} %fusion.41), calls=%async_computation.2 | async-start | bytes 3211264 | tf_op jit(solution)/shard_map/slice | solution.py:418
  28.3 2.6 %copy-start.10 = (f32[64,32,49]{2,1,0:T(8,128)S(1)}, f32[64,32,49]{2,1,0:T(8,128)}, u32[]{:S(2)}) copy-start(f32[64,32,49]{2,1,0:T(8,128)} %copy.44) | copy-start | bytes 1204228
  31.0 14.5 %copy-start.4 = (f32[64,81,128]{2,0,1:T(8,128)S(1)}, f32[64,81,128]{2,0,1:T(8,128)}, u32[]{:S(2)}) copy-start(f32[64,81,128]{2,0,1:T(8,128)} %fusion.41) | copy-start | bytes 7962628
  47.4 63.4 %collective-permute-start.2 = (f32[96,49,128]{2,0,1:T(8,128)}, f32[96,49,128]{2,0,1:T(8,128)S(1)}, u32[]{:S(2)}, u32[]{:S(2)}) collective-permute-start(f32[96,49,128]{2,0,1:T(8,128)} %maximum_maximum_fusion), channel_id=1, source_target_pairs={{0,16},{16,0},{1,17},{17,1},{2,18},{18,2},{3,19},{19,3},{4,20},{20... | collective-permute-start | bytes 7225352 | tf_op jit(solution)/shard_map/ppermute | solution.py:434
  105.6 25.0 %collective-permute-start.3 = (f32[64,32,128]{2,0,1:T(8,128)}, f32[64,32,128]{2,0,1:T(8,128)}, u32[]{:S(2)}, u32[]{:S(2)}) collective-permute-start(f32[64,32,128]{2,0,1:T(8,128)} %convolution_bitcast_fusion), channel_id=1, source_target_pairs={{0,16},{16,0},{1,17},{17,1},{2,18},{18,2},{3,19},{19,3},{4,20},{20... | collective-permute-start | bytes 3145736 | tf_op jit(solution)/shard_map/ppermute | solution.py:440
  111.1 1.8 %copy-start.5 = (f32[64,81,128]{2,0,1:T(8,128)S(1)}, f32[64,81,128]{2,0,1:T(8,128)}, u32[]{:S(2)}) copy-start(f32[64,81,128]{2,0,1:T(8,128)} %fusion.41) | copy-start | bytes 7962628
  111.1 1.7 %copy-start.16 = (f32[128,128]{1,0:T(8,128)S(1)}, f32[128,128]{1,0:T(8,128)}, u32[]{:S(2)}) copy-start(f32[128,128]{1,0:T(8,128)} %copy-done.15) | copy-start | bytes 196612
  112.9 1.5 %copy-start.6 = (f32[64,49,49]{2,1,0:T(8,128)S(1)}, f32[64,49,49]{2,1,0:T(8,128)}, u32[]{:S(2)}) copy-start(f32[64,49,49]{2,1,0:T(8,128)} %copy.54) | copy-start | bytes 1843972
  114.4 2.4 %copy-start.11 = (f32[64,32,49]{2,1,0:T(8,128)S(1)}, f32[64,32,49]{2,1,0:T(8,128)}, u32[]{:S(2)}) copy-start(f32[64,32,49]{2,1,0:T(8,128)} %copy.44) | copy-start | bytes 1204228
  114.4 2.4 %copy-start.25 = (f32[128]{0:T(128)S(1)}, f32[128]{0:T(128)}, u32[]{:S(2)}) copy-start(f32[128]{0:T(128)} %param.12) | copy-start | bytes 1540
  116.8 3.4 %copy-start.12 = (f32[64,32,128]{2,1,0:T(8,128)S(1)}, f32[64,32,128]{2,1,0:T(8,128)}, u32[]{:S(2)}) copy-start(f32[64,32,128]{2,1,0:T(8,128)} %copy.58) | copy-start | bytes 3145732
  120.2 1.8 %copy-start.2 = (f32[64,81,128]{2,0,1:T(8,128)S(1)}, f32[64,81,128]{2,0,1:T(8,128)}, u32[]{:S(2)}) copy-start(f32[64,81,128]{2,0,1:T(8,128)} %copy-done) | copy-start | bytes 7962628
  124.4 6.2 %copy-start.9 = (f32[64,16,49]{2,1,0:T(8,128)S(1)}, f32[64,16,49]{2,1,0:T(8,128)}, u32[]{:S(2)}) copy-start(f32[64,16,49]{2,1,0:T(8,128)} %copy-done.8) | copy-start | bytes 602116
